TPU v7x, 32 devices: a whole 2x2x4 slice. The times are simulated.
32 devices in a mesh: wide: 4 (over y, x), narrow: 8 (over z, core).
Axes of the slice: x: 2, y: 2, z: 4, core: 2. Of those that a mesh axis runs over, the one named last changes fastest.
Arguments:
- amplitudes: bfloat16 [1024, 65536], P('narrow', 'wide'), may hold values from -6 to 6
- ladder_ints: bfloat16 [65536, 8192], P('wide', 'narrow'), may hold values from -0.0234375 to 0.0234375
- cycle_amps: bfloat16 [1024, 8192], P('wide', 'narrow'), may hold values from -6 to 6
- cycle_ints: bfloat16 [8192, 8192], P('narrow', 'wide'), may hold values from -0.0625 to 0.0625
Outputs:
- residual: bfloat16 [32, 32, 32, 256], P('wide', None, 'narrow')
All inputs are finite; a program needn't handle non-finite values.
Results may differ from a plain program's by a relative error of at most 0.001.
Values may be sent and summed in bfloat16 or wider, within the bound.
A program may use at most 128 MiB of HBM per device.

v0:
```python
import jax
import jax.numpy as jnp
from jax import lax
from jax.sharding import PartitionSpec as P

OCC = 32
VIRT = 256
WINDOW = 32


def per_device(amplitudes, ladder_ints, cycle_amps, cycle_ints):
    window_local = ladder_ints.shape[1] // VIRT
    ladder = jnp.dot(
        lax.all_gather(amplitudes, "narrow", axis=0, tiled=True),
        ladder_ints,
        preferred_element_type=jnp.float32,
    )
    ladder = ladder.reshape(OCC, OCC, window_local, VIRT)
    ladder = lax.psum_scatter(ladder, "wide", scatter_dimension=0, tiled=True)
    cycle = jnp.dot(
        lax.all_gather(cycle_amps, "wide", axis=0, tiled=True),
        cycle_ints,
        preferred_element_type=jnp.float32,
    )
    occ_local = cycle.shape[1] // VIRT
    cycle = cycle.reshape(OCC, WINDOW, occ_local, VIRT)
    cycle = lax.psum_scatter(cycle, "narrow", scatter_dimension=1, tiled=True)
    total = ladder + jnp.transpose(cycle, (2, 0, 1, 3))
    return total.astype(jnp.bfloat16)


def solution(mesh):
    in_specs = (P("narrow", "wide"), P("wide", "narrow"), P("wide", "narrow"), P("narrow", "wide"))
    out_specs = P("wide", None, "narrow", None)
    return jax.shard_map(
        per_device, mesh=mesh, in_specs=in_specs, out_specs=out_specs, check_vma=False
    )
```

profile of v0, /device:TPU:0, one launch (start us, length us, event | category | flops | bytes accessed | tf_op | source)
XLA Modules:
  0.0 490.9 jit_solution(8458095031129911044)
XLA Ops:
  6.5 0.0 all-gather.5.cloned.1.call-start
  6.5 0.7 all-gather.5.cloned.1.call-update
  7.3 0.0 all-gather.3.cloned.1.call-start
  7.3 0.7 all-gather.3.cloned.1.call-update
  8.0 0.0 reduce-scatter.5.cloned.1.call-start
  8.1 39.1 %all-gather.5.cloned.1.call-done = bf16[1024,1024]{1,0:T(8,128)(2,1)} async-done(((bf16[256,1024]{1,0:T(8,128)(2,1)}), bf16[1024,1024]{1,0:T(8,128)(2,1)}) %all-gather.5.cloned.1.call-update) | async-done | bytes 2097168 | tf_op jit(solution)/shard_map/all_gather | solution.py:21
  47.1 6.9 %fusion.2 = f32[1024,2048]{1,0:T(8,128)S(1)} fusion(bf16[1024,1024]{1,0:T(8,128)(2,1)} %all-gather.5.cloned.1.call-done, bf16[1024,2048]{1,0:T(8,128)(2,1)} %param.7), kind=kOutput, calls=%fused_computation.3 | convolution fusion | flops 4294967296 | bytes 14680064 | tf_op jit(solution)/shard_map/dot_general | solution.py:20
  54.0 4.1 copy.10
  58.1 5.3 %copy.7 = f32[32,32,8,256]{3,2,0,1:T(8,128)} copy(f32[32,32,8,256]{3,2,1,0:T(8,128)S(1)} %bitcast.11) | data formatting | bytes 16777216 | tf_op jit(solution)/shard_map/reshape | solution.py:26
  63.5 0.0 reduce-scatter.5.cloned.1.call-update
  63.5 0.2 reduce-scatter.3.cloned.1.call-start
  63.7 273.6 %all-gather.3.cloned.1.call-done = bf16[1024,16384]{1,0:T(8,128)(2,1)} async-done(((bf16[128,16384]{1,0:T(8,128)(2,1)}), bf16[1024,16384]{1,0:T(8,128)(2,1)}) %all-gather.3.cloned.1.call-update) | async-done | bytes 33554448 | tf_op jit(solution)/shard_map/all_gather | solution.py:14
  337.3 41.6 %fusion.1 = f32[1024,1024]{1,0:T(8,128)} fusion(bf16[1024,16384]{1,0:T(8,128)(2,1)} %all-gather.3.cloned.1.call-done, bf16[16384,1024]{1,0:T(8,128)(2,1)} %param.5), kind=kOutput, calls=%fused_computation.2 | convolution fusion | flops 34359738368 | bytes 71303168 | tf_op jit(solution)/shard_map/dot_general | solution.py:13
  379.0 5.7 %reshape.6 = f32[32,32,4,256]{3,2,1,0:T(4,128)} reshape(f32[1024,1024]{1,0:T(8,128)} %fusion.1) | data formatting | bytes 8388608 | tf_op jit(solution)/shard_map/reshape | solution.py:18
  384.6 5.0 %copy.6 = f32[32,32,4,256]{3,1,2,0:T(8,128)} copy(f32[32,32,4,256]{3,2,1,0:T(4,128)} %reshape.6) | data formatting | bytes 8388608 | tf_op jit(solution)/shard_map/reshape | solution.py:18
  389.6 0.0 reduce-scatter.3.cloned.1.call-update
  389.7 37.7 %reduce-scatter.5.cloned.1.call-done = f32[32,4,8,256]{3,2,0,1:T(8,128)} async-done(((f32[32,32,8,256]{3,2,0,1:T(8,128)}), f32[32,4,8,256]{3,2,0,1:T(8,128)}) %reduce-scatter.5.cloned.1.call-update) | async-done | bytes 1048592 | tf_op jit(solution)/shard_map/reduce_scatter | solution.py:27
  427.4 53.9 %reduce-scatter.3.cloned.1.call-done = f32[8,32,4,256]{3,1,2,0:T(8,128)} async-done(((f32[32,32,4,256]{3,1,2,0:T(8,128)}), f32[8,32,4,256]{3,1,2,0:T(8,128)}) %reduce-scatter.3.cloned.1.call-update) | async-done | bytes 1048592 | tf_op jit(solution)/shard_map/reduce_scatter | solution.py:19
  481.3 1.9 fusion
  483.2 1.2 copy.9
Async XLA Ops:
  6.5 40.6 %all-gather.5.cloned.1.call-start = ((), (), s32[]{:S(2)}) async-start(), calls=%async_computation.4 | async-start | bytes 2621440 | tf_op jit(solution)/shard_map/all_gather | solution.py:21
  7.3 330.1 %all-gather.3.cloned.1.call-start = ((), (), s32[]{:S(2)}) async-start(), calls=%async_computation.2 | async-start | bytes 37748736 | tf_op jit(solution)/shard_map/all_gather | solution.py:14
  8.0 419.4 %reduce-scatter.5.cloned.1.call-start = ((), (), s32[]{:S(2)}) async-start(), calls=%async_computation.5 | async-start | bytes 9437184 | tf_op jit(solution)/shard_map/reduce_scatter | solution.py:27
  63.5 417.8 %reduce-scatter.3.cloned.1.call-start = ((), (), s32[]{:S(2)}) async-start(), calls=%async_computation.3 | async-start | bytes 5242880 | tf_op jit(solution)/shard_map/reduce_scatter | solution.py:19
Sparse Core Ops, SparseCore 0:
  9.2 37.8 all-gather.4
  48.7 288.5 all-gather.2
  339.6 87.6 reduce-scatter.4
  430.2 51.0 reduce-scatter.2
where the time goes:
time: 491 us
  waiting for transfers between devices  406 us (83%)
  matrix products  48.5 us (10%)
  local copies, waits for them, and re-layouts  21.3 us (4%)
  between operations  13.1 us (3%)
    all_gather x1, waiting for transfers between devices, per_device(): lax.all_gather(amplitudes, 'narrow', axis=0, tiled=True)  274 us
    reduce_scatter x1, waiting for transfers between devices, per_device(): ladder = lax.psum_scatter(ladder, 'wide', scatter_dimension=0, tiled=True)  53.9 us
    dot_general x1, matrix products, per_device(): jnp.dot(lax.all_gather(amplitudes, 'narrow', axis=0, tiled=True), ladder_...  41.6 us
    all_gather x1, waiting for transfers between devices, per_device(): lax.all_gather(cycle_amps, 'wide', axis=0, tiled=True)  39.1 us
    reduce_scatter x1, waiting for transfers between devices, per_device(): cycle = lax.psum_scatter(cycle, 'narrow', scatter_dimension=1, tiled=True)  37.7 us
    reshape x2, local copies, waits for them, and re-layouts, per_device(): ladder = ladder.reshape(OCC, OCC, window_local, VIRT)  10.7 us
  transfers between devices with their start and end apart: 4, of which 4 were waited for; matrix products, arithmetic and copies ran while one was open for 14% of the time, Pallas kernels for 0%

commit v1 on v0

v1 whole, which is shorter than its diff:
```python
import jax
import jax.numpy as jnp
from jax import lax
from jax.sharding import PartitionSpec as P

OCC = 32
VIRT = 256
WINDOW = 32
CHUNKS = 4


def gather_rows(block, axis, size):
    if size > 4:
        return lax.all_gather(block, axis, axis=1)
    me = lax.axis_index(axis)
    shape = (block.shape[0], size) + block.shape[1:]
    out = jnp.zeros(shape, block.dtype)
    out = lax.dynamic_update_slice_in_dim(out, block[:, None], me, 1)
    for shift in range(1, size):
        pairs = [(d, (d + shift) % size) for d in range(size)]
        got = lax.ppermute(block, axis, pairs)
        out = lax.dynamic_update_slice_in_dim(out, got[:, None], lax.rem(me + size - shift, size), 1)
    return out


def scatter_sum(partial, axis, size, low_first):
    bits = size.bit_length() - 1
    me = lax.axis_index(axis)
    rows, cols = partial.shape
    held = partial.reshape((2,) * bits + (rows // size, cols))
    left = list(range(bits - 1, -1, -1))
    for bit in list(range(bits)) if low_first else list(range(bits - 1, -1, -1)):
        where = left.index(bit)
        left.remove(bit)
        mine = lax.rem(lax.div(me, 1 << bit), 2)
        keep = lax.dynamic_index_in_dim(held, mine, where, keepdims=False)
        send = lax.dynamic_index_in_dim(held, 1 - mine, where, keepdims=False)
        held = keep + lax.ppermute(send, axis, [(d, d ^ (1 << bit)) for d in range(size)])
    return held


def solution(mesh):
    wide, narrow = mesh.shape["wide"], mesh.shape["narrow"]

    def per_device(amplitudes, ladder_ints, cycle_amps, cycle_ints):
        window_local = ladder_ints.shape[1] // VIRT
        occ_rows = amplitudes.shape[0] // OCC
        occ_local = cycle_ints.shape[1] // VIRT
        chunks = min(CHUNKS, occ_rows)
        rows = amplitudes.shape[0] // chunks
        per_chunk = occ_rows // chunks

        depth = cycle_amps.shape[1]
        local = cycle_amps.reshape(-1, narrow, window_local, depth)
        local = jnp.transpose(local, (1, 0, 2, 3)).reshape(narrow, -1, depth)
        everyone = gather_rows(local, "wide", wide).reshape(-1, depth)

        gathered = []
        for c in range(chunks):
            block = amplitudes[c * rows : (c + 1) * rows]
            gathered.append(lax.all_gather(block, "narrow", axis=0, tiled=True))

        cycle = jnp.dot(everyone, cycle_ints, preferred_element_type=jnp.float32)
        cycle = lax.psum_scatter(cycle, "narrow", scatter_dimension=0, tiled=True)

        pieces = []
        for c in range(chunks):
            ladder = jnp.dot(gathered[c], ladder_ints, preferred_element_type=jnp.float32)
            half = ladder.shape[1] // 2
            if wide & (wide - 1) or narrow % wide or half % VIRT:
                piece = lax.psum_scatter(ladder, "wide", scatter_dimension=0, tiled=True)
            else:
                piece = jnp.concatenate(
                    [
                        scatter_sum(ladder[:, :half], "wide", wide, False),
                        scatter_sum(ladder[:, half:], "wide", wide, True),
                    ],
                    axis=1,
                )
            pieces.append(piece.reshape(narrow // wide, per_chunk, OCC, window_local, VIRT))
        ladder = jnp.stack(pieces, axis=1).reshape(occ_local, OCC, window_local, VIRT)
        cycle = cycle.reshape(OCC, window_local, occ_local, VIRT)
        total = ladder + jnp.transpose(cycle, (2, 0, 1, 3))
        return total.astype(jnp.bfloat16)

    in_specs = (P("narrow", "wide"), P("wide", "narrow"), P("wide", "narrow"), P("narrow", "wide"))
    out_specs = P("wide", None, "narrow", None)
    return jax.shard_map(
        per_device, mesh=mesh, in_specs=in_specs, out_specs=out_specs, check_vma=False
    )
```

time: 491 us -> 442 us (0.900)
  waiting for transfers between devices: 406 us -> 296 us
  matrix products: 48.5 us -> 83.8 us
  starting transfers between devices: 0.3 us -> 27.2 us
  local copies, waits for them, and re-layouts: 21.3 us -> 13.8 us
  other arithmetic: 1.88 us -> 6.96 us
    all_gather x2 -> x4, waiting for transfers between devices: 313 us -> 224 us  [per_device(): gathered.append(lax.all_gather(block, 'narrow', axis=0, tiled=True))]
    reduce_scatter x2 -> x1, waiting for transfers between devices: 91.6 us -> 45.6 us  [per_device(): cycle = lax.psum_scatter(cycle, 'narrow', scatter_dimension=0, tiled=True)]
    dot_general x2 -> x5, matrix products: 48.5 us -> 83.8 us  [the longest x4 74.7 us: per_device(): jnp.dot(gathered[c], ladder_ints, preferred_element_type=jnp.float32)]
    ppermute x0 -> x19, starting transfers between devices: none -> 27.1 us  [the longest x16 21.1 us: scatter_sum(): lax.ppermute(send, axis, [(d, d ^ 1 << bit) for d in range(size)])]
    ppermute x0 -> x19, waiting for transfers between devices: none -> 25.4 us  [the longest x3 19.3 us: gather_rows(): got = lax.ppermute(block, axis, pairs)]
    reshape x3 -> x1, local copies, waits for them, and re-layouts: 16 us -> 0.2 us  [per_device(): local = cycle_amps.reshape(-1, narrow, window_local, depth)]
    add x0 -> x16, other arithmetic: none -> 5.22 us  [scatter_sum(): keep + lax.ppermute(send, axis, [(d, d ^ 1 << bit) for d in range(size)])]
  transfers between devices with their start and end apart: 4 -> 24, of which waited for: 4 -> 12; matrix products, arithmetic and copies ran while one was open for 14% -> 22% of each run, Pallas kernels for 0% -> 0%
where the time goes in v1:
time: 442 us
  waiting for transfers between devices  296 us (67%)
  matrix products  83.8 us (19%)
  starting transfers between devices  27.2 us (6%)
  local copies, waits for them, and re-layouts  13.8 us (3%)
  between operations  13.6 us (3%)
  other arithmetic  6.96 us (2%)
    all_gather x4, waiting for transfers between devices, per_device(): gathered.append(lax.all_gather(block, 'narrow', axis=0, tiled=True))  224 us
    dot_general x4, matrix products, per_device(): jnp.dot(gathered[c], ladder_ints, preferred_element_type=jnp.float32)  74.7 us
    reduce_scatter x1, waiting for transfers between devices, per_device(): cycle = lax.psum_scatter(cycle, 'narrow', scatter_dimension=0, tiled=True)  45.6 us
    ppermute x16, starting transfers between devices, scatter_sum(): lax.ppermute(send, axis, [(d, d ^ 1 << bit) for d in range(size)])  21.1 us
    ppermute x3, waiting for transfers between devices, gather_rows(): got = lax.ppermute(block, axis, pairs)  19.3 us
    dot_general x1, matrix products, per_device(): cycle = jnp.dot(everyone, cycle_ints, preferred_element_type=jnp.float32)  9.09 us
  transfers between devices with their start and end apart: 24, of which 12 were waited for; matrix products, arithmetic and copies ran while one was open for 22% of the time, Pallas kernels for 0%

profile of v1, /device:TPU:0, one launch (start us, length us, event | category | flops | bytes accessed | tf_op | source)
XLA Modules:
  0.0 441.8 jit_solution(4430023894371799846)
XLA Ops:
  6.5 4.4 fusion.1
  11.0 0.7 all-gather.9.cloned.1.call-update
  11.7 0.7 all-gather.7.cloned.1.call-update
  13.4 3.0 collective-permute-start.16
  16.4 1.5 collective-permute-start.17
  17.9 1.4 collective-permute-start.18
  20.0 10.3 %collective-permute-done.16 = bf16[8,32,1024]{2,0,1:T(8,128)(2,1)} collective-permute-done((bf16[8,32,1024]{2,0,1:T(8,128)(2,1)S(1)}, bf16[8,32,1024]{2,0,1:T(8,128)(2,1)}, u32[]{:S(2)}, u32[]{:S(2)}) %collective-permute-start.16) | collective-permute-done | bytes 524320 | tf_op jit(solution)/shard_map/ppermute | solution.py:21
  30.3 1.4 copy_dynamic-update-slice_fusion.2
  31.7 9.0 %collective-permute-done.17 = bf16[8,32,1024]{2,0,1:T(8,128)(2,1)} collective-permute-done((bf16[8,32,1024]{2,0,1:T(8,128)(2,1)S(1)}, bf16[8,32,1024]{2,0,1:T(8,128)(2,1)}, u32[]{:S(2)}, u32[]{:S(2)}) %collective-permute-start.17) | collective-permute-done | bytes 524320 | tf_op jit(solution)/shard_map/ppermute | solution.py:21
  40.6 1.4 copy_dynamic-update-slice_fusion.1
  42.3 9.1 %fusion.10 = f32[1024,2048]{1,0:T(8,128)} fusion(bf16[1024,1024]{1,0:T(8,128)(2,1)S(1)} %bitcast.99, bf16[1024,2048]{1,0:T(8,128)(2,1)} %param.7), kind=kOutput, calls=%fused_computation.52 | convolution fusion | flops 4294967296 | bytes 14680064 | tf_op jit(solution)/shard_map/dot_general | solution.py:63
  51.5 44.4 %all-gather.11.cloned.1.call-done = bf16[256,16384]{1,0:T(8,128)(2,1)} async-done(((bf16[32,16384]{1,0:T(8,128)(2,1)}), bf16[256,16384]{1,0:T(8,128)(2,1)}) %all-gather.11.cloned.1.call-update) | async-done | bytes 8388624 | tf_op jit(solution)/shard_map/all_gather | solution.py:61
  95.8 18.8 %fusion.9 = f32[256,1024]{1,0:T(8,128)S(1)} fusion(bf16[256,16384]{1,0:T(8,128)(2,1)} %all-gather.11.cloned.1.call-done, bf16[16384,1024]{1,0:T(8,128)(2,1)} %param.5), kind=kOutput, calls=%fused_computation.51 | convolution fusion | flops 8589934592 | bytes 42991616 | tf_op jit(solution)/shard_map/dot_general | solution.py:68
  114.8 0.7 dynamic-slice_bitcast_fusion
  115.5 1.5 collective-permute-start.14
  117.0 1.5 collective-permute-start.12
  118.5 59.5 %all-gather.9.cloned.1.call-done = bf16[256,16384]{1,0:T(8,128)(2,1)} async-done(((bf16[32,16384]{1,0:T(8,128)(2,1)}), bf16[256,16384]{1,0:T(8,128)(2,1)}) %all-gather.9.cloned.1.call-update) | async-done | bytes 8388624 | tf_op jit(solution)/shard_map/all_gather | solution.py:61
  178.0 18.8 %fusion.8 = f32[256,1024]{1,0:T(8,128)S(1)} fusion(bf16[256,16384]{1,0:T(8,128)(2,1)} %all-gather.9.cloned.1.call-done, bf16[16384,1024]{1,0:T(8,128)(2,1)} %param.5), kind=kOutput, calls=%fused_computation.50 | convolution fusion | flops 8589934592 | bytes 42991616 | tf_op jit(solution)/shard_map/dot_general | solution.py:68
  196.9 0.7 dynamic-slice_bitcast_fusion.2
  197.6 1.5 collective-permute-start.10
  199.1 0.7 dynamic-slice_bitcast_fusion.3
  199.8 1.5 collective-permute-start.8
  201.3 58.9 %all-gather.7.cloned.1.call-done = bf16[256,16384]{1,0:T(8,128)(2,1)} async-done(((bf16[32,16384]{1,0:T(8,128)(2,1)}), bf16[256,16384]{1,0:T(8,128)(2,1)}) %all-gather.7.cloned.1.call-update) | async-done | bytes 8388624 | tf_op jit(solution)/shard_map/all_gather | solution.py:61
  260.1 18.8 %fusion.7 = f32[256,1024]{1,0:T(8,128)S(1)} fusion(bf16[256,16384]{1,0:T(8,128)(2,1)} %all-gather.7.cloned.1.call-done, bf16[16384,1024]{1,0:T(8,128)(2,1)} %param.5), kind=kOutput, calls=%fused_computation.49 | convolution fusion | flops 8589934592 | bytes 42991616 | tf_op jit(solution)/shard_map/dot_general | solution.py:68
  279.1 0.7 dynamic-slice_bitcast_fusion.4
  279.8 1.5 collective-permute-start.6
  281.3 60.9 %all-gather.5.cloned.1.call-done = bf16[256,16384]{1,0:T(8,128)(2,1)} async-done(((bf16[32,16384]{1,0:T(8,128)(2,1)}), bf16[256,16384]{1,0:T(8,128)(2,1)}) %all-gather.5.cloned.1.call-update) | async-done | bytes 8388624 | tf_op jit(solution)/shard_map/all_gather | solution.py:61
  342.2 18.2 %fusion.6 = f32[256,1024]{1,0:T(8,128)S(1)} fusion(bf16[256,16384]{1,0:T(8,128)(2,1)} %all-gather.5.cloned.1.call-done, bf16[16384,1024]{1,0:T(8,128)(2,1)} %param.5), kind=kOutput, calls=%fused_computation.48 | convolution fusion | flops 8589934592 | bytes 42991616 | tf_op jit(solution)/shard_map/dot_general | solution.py:68
  360.6 1.5 collective-permute-start.4
  362.1 1.0 bitcast_add_fusion.1
  363.1 1.5 collective-permute-start.2
  364.6 1.0 bitcast_add_fusion.3
  366.3 1.0 bitcast_add_fusion.2
  367.3 1.5 collective-permute-start.15
  368.8 1.0 bitcast_add_fusion.4
  370.5 1.0 bitcast_add_fusion.5
  372.2 1.5 collective-permute-start.9
  373.8 1.6 collective-permute-done
  375.4 1.5 collective-permute-start.7
  377.0 1.2 collective-permute-done.15
  378.2 1.5 collective-permute-start.5
  379.7 1.5 collective-permute-start.3
  381.3 1.2 collective-permute-start.1
  382.6 1.3 collective-permute-done.7
  384.4 1.6 collective-permute-done.3
  386.8 45.6 %reduce-scatter.2.cloned.1.call-done = f32[128,2048]{1,0:T(8,128)} async-done(((f32[1024,2048]{1,0:T(8,128)}), f32[128,2048]{1,0:T(8,128)}) %reduce-scatter.2.cloned.1.call-update) | async-done | bytes 1048592 | tf_op jit(solution)/shard_map/reduce_scatter | solution.py:64
  432.3 1.6 copy.16
  433.9 1.4 fusion
  (67 shorter events, 5.8 us)
Async XLA Ops:
  6.5 6.5 %copy-start = (bf16[256,1024]{1,0:T(8,128)(2,1)S(1)}, bf16[256,1024]{1,0:T(8,128)(2,1)}, u32[]{:S(2)}) copy-start(bf16[256,1024]{1,0:T(8,128)(2,1)} %param.6) | copy-start | bytes 1572868
  6.5 89.3 %all-gather.11.cloned.1.call-start = ((), (), s32[]{:S(2)}) async-start(), calls=%async_computation.4 | async-start | bytes 9437184 | tf_op jit(solution)/shard_map/all_gather | solution.py:61
  10.9 167.1 %all-gather.9.cloned.1.call-start = ((), (), s32[]{:S(2)}) async-start(), calls=%async_computation.3 | async-start | bytes 9437184 | tf_op jit(solution)/shard_map/all_gather | solution.py:61
  11.7 248.5 %all-gather.7.cloned.1.call-start = ((), (), s32[]{:S(2)}) async-start(), calls=%async_computation.2 | async-start | bytes 9437184 | tf_op jit(solution)/shard_map/all_gather | solution.py:61
  12.4 329.7 %all-gather.5.cloned.1.call-start = ((), (), s32[]{:S(2)}) async-start(), calls=%async_computation.1 | async-start | bytes 9437184 | tf_op jit(solution)/shard_map/all_gather | solution.py:61
  13.0 419.4 %reduce-scatter.2.cloned.1.call-start = ((), (), s32[]{:S(2)}) async-start(), calls=%async_computation.5 | async-start | bytes 9437184 | tf_op jit(solution)/shard_map/reduce_scatter | solution.py:64
  13.4 16.9 %collective-permute-start.16 = (bf16[8,32,1024]{2,0,1:T(8,128)(2,1)S(1)}, bf16[8,32,1024]{2,0,1:T(8,128)(2,1)}, u32[]{:S(2)}, u32[]{:S(2)}) collective-permute-start(bf16[8,32,1024]{2,0,1:T(8,128)(2,1)S(1)} %bitcast.100), channel_id=1, source_target_pairs={{0,8},{8,16},{16,24},{24,0},{1,9},{9,17},{17,25},{25,1},{2,10},{10... | collective-permute-start | bytes 1572872 | tf_op jit(solution)/shard_map/ppermute | solution.py:21
  16.4 24.2 %collective-permute-start.17 = (bf16[8,32,1024]{2,0,1:T(8,128)(2,1)S(1)}, bf16[8,32,1024]{2,0,1:T(8,128)(2,1)}, u32[]{:S(2)}, u32[]{:S(2)}) collective-permute-start(bf16[8,32,1024]{2,0,1:T(8,128)(2,1)S(1)} %bitcast.101), channel_id=1, source_target_pairs={{0,16},{8,24},{16,0},{24,8},{1,17},{9,25},{17,1},{25,9},{2,18},{10... | collective-permute-start | bytes 1572872 | tf_op jit(solution)/shard_map/ppermute | solution.py:21
  17.9 24.1 %collective-permute-start.18 = (bf16[8,32,1024]{2,0,1:T(8,128)(2,1)S(1)}, bf16[8,32,1024]{2,0,1:T(8,128)(2,1)S(1)}, u32[]{:S(2)}, u32[]{:S(2)}) collective-permute-start(bf16[8,32,1024]{2,0,1:T(8,128)(2,1)S(1)} %bitcast.102), channel_id=1, source_target_pairs={{0,24},{8,0},{16,8},{24,16},{1,25},{9,1},{17,9},{25,17},{2,26},{10... | collective-permute-start | bytes 1572872 | tf_op jit(solution)/shard_map/ppermute | solution.py:21
  115.5 245.1 %collective-permute-start.14 = (f32[2,64,512]{2,1,0:T(8,128)}, f32[2,64,512]{2,1,0:T(8,128)}, u32[]{:S(2)}, u32[]{:S(2)}) collective-permute-start(f32[2,64,512]{2,1,0:T(8,128)} %dynamic-slice_bitcast_fusion), channel_id=1, source_target_pairs={{0,8},{8,0},{16,24},{24,16},{1,9},{9,1},{17,25},{25,17},{2,10},{10... | collective-permute-start | bytes 786440 | tf_op jit(solution)/shard_map/ppermute | solution.py:38
  117.0 248.7 %collective-permute-start.12 = (f32[2,64,512]{2,1,0:T(8,128)S(1)}, f32[2,64,512]{2,1,0:T(8,128)}, u32[]{:S(2)}, u32[]{:S(2)}) collective-permute-start(f32[2,64,512]{2,1,0:T(8,128)S(1)} %dynamic-slice_bitcast_fusion.1), channel_id=1, source_target_pairs={{0,16},{8,24},{16,0},{24,8},{1,17},{9,25},{17,1},{25,9},{2,18},{10... | collective-permute-start | bytes 786440 | tf_op jit(solution)/shard_map/ppermute | solution.py:38
  197.6 165.5 %collective-permute-start.10 = (f32[2,64,512]{2,1,0:T(8,128)}, f32[2,64,512]{2,1,0:T(8,128)}, u32[]{:S(2)}, u32[]{:S(2)}) collective-permute-start(f32[2,64,512]{2,1,0:T(8,128)} %dynamic-slice_bitcast_fusion.2), channel_id=1, source_target_pairs={{0,8},{8,0},{16,24},{24,16},{1,9},{9,1},{17,25},{25,17},{2,10},{10... | collective-permute-start | bytes 786440 | tf_op jit(solution)/shard_map/ppermute | solution.py:38
  199.8 167.5 %collective-permute-start.8 = (f32[2,64,512]{2,1,0:T(8,128)}, f32[2,64,512]{2,1,0:T(8,128)}, u32[]{:S(2)}, u32[]{:S(2)}) collective-permute-start(f32[2,64,512]{2,1,0:T(8,128)} %dynamic-slice_bitcast_fusion.3), channel_id=1, source_target_pairs={{0,16},{8,24},{16,0},{24,8},{1,17},{9,25},{17,1},{25,9},{2,18},{10... | collective-permute-start | bytes 786440 | tf_op jit(solution)/shard_map/ppermute | solution.py:38
  279.8 90.1 %collective-permute-start.6 = (f32[2,64,512]{2,1,0:T(8,128)}, f32[2,64,512]{2,1,0:T(8,128)}, u32[]{:S(2)}, u32[]{:S(2)}) collective-permute-start(f32[2,64,512]{2,1,0:T(8,128)} %dynamic-slice_bitcast_fusion.4), channel_id=1, source_target_pairs={{0,8},{8,0},{16,24},{24,16},{1,9},{9,1},{17,25},{25,17},{2,10},{10... | collective-permute-start | bytes 786440 | tf_op jit(solution)/shard_map/ppermute | solution.py:38
  360.6 10.9 %collective-permute-start.4 = (f32[2,64,512]{2,1,0:T(8,128)S(1)}, f32[2,64,512]{2,1,0:T(8,128)S(1)}, u32[]{:S(2)}, u32[]{:S(2)}) collective-permute-start(f32[2,64,512]{2,1,0:T(8,128)S(1)} %dynamic-slice_bitcast_fusion.5), channel_id=1, source_target_pairs={{0,16},{8,24},{16,0},{24,8},{1,17},{9,25},{17,1},{25,9},{2,18},{10... | collective-permute-start | bytes 786440 | tf_op jit(solution)/shard_map/ppermute | solution.py:38
  363.1 9.1 %collective-permute-start.2 = (f32[2,64,512]{2,1,0:T(8,128)S(1)}, f32[2,64,512]{2,1,0:T(8,128)S(1)}, u32[]{:S(2)}, u32[]{:S(2)}) collective-permute-start(f32[2,64,512]{2,1,0:T(8,128)S(1)} %dynamic-slice_bitcast_fusion.6), channel_id=1, source_target_pairs={{0,8},{8,0},{16,24},{24,16},{1,9},{9,1},{17,25},{25,17},{2,10},{10... | collective-permute-start | bytes 786440 | tf_op jit(solution)/shard_map/ppermute | solution.py:38
  365.7 9.8 %collective-permute-start = (f32[2,64,512]{2,1,0:T(8,128)S(1)}, f32[2,64,512]{2,1,0:T(8,128)S(1)}, u32[]{:S(2)}, u32[]{:S(2)}) collective-permute-start(f32[2,64,512]{2,1,0:T(8,128)S(1)} %dynamic-slice_bitcast_fusion.7), channel_id=1, source_target_pairs={{0,16},{8,24},{16,0},{24,8},{1,17},{9,25},{17,1},{25,9},{2,18},{10... | collective-permute-start | bytes 786440 | tf_op jit(solution)/shard_map/ppermute | solution.py:38
  367.3 11.0 %collective-permute-start.15 = (f32[64,512]{1,0:T(8,128)S(1)}, f32[64,512]{1,0:T(8,128)S(1)}, u32[]{:S(2)}, u32[]{:S(2)}) collective-permute-start(f32[64,512]{1,0:T(8,128)S(1)} %dynamic-slice_bitcast_fusion.8), channel_id=1, source_target_pairs={{0,16},{8,24},{16,0},{24,8},{1,17},{9,25},{17,1},{25,9},{2,18},{10... | collective-permute-start | bytes 393224 | tf_op jit(solution)/shard_map/ppermute | solution.py:38
  369.9 9.8 %collective-permute-start.13 = (f32[64,512]{1,0:T(8,128)S(1)}, f32[64,512]{1,0:T(8,128)S(1)}, u32[]{:S(2)}, u32[]{:S(2)}) collective-permute-start(f32[64,512]{1,0:T(8,128)S(1)} %dynamic-slice_bitcast_fusion.9), channel_id=1, source_target_pairs={{0,8},{8,0},{16,24},{24,16},{1,9},{9,1},{17,25},{25,17},{2,10},{10... | collective-permute-start | bytes 393224 | tf_op jit(solution)/shard_map/ppermute | solution.py:38
  371.5 9.8 %collective-permute-start.11 = (f32[64,512]{1,0:T(8,128)S(1)}, f32[64,512]{1,0:T(8,128)S(1)}, u32[]{:S(2)}, u32[]{:S(2)}) collective-permute-start(f32[64,512]{1,0:T(8,128)S(1)} %dynamic-slice_bitcast_fusion.10), channel_id=1, source_target_pairs={{0,16},{8,24},{16,0},{24,8},{1,17},{9,25},{17,1},{25,9},{2,18},{10... | collective-permute-start | bytes 393224 | tf_op jit(solution)/shard_map/ppermute | solution.py:38
  372.2 10.3 %collective-permute-start.9 = (f32[64,512]{1,0:T(8,128)S(1)}, f32[64,512]{1,0:T(8,128)S(1)}, u32[]{:S(2)}, u32[]{:S(2)}) collective-permute-start(f32[64,512]{1,0:T(8,128)S(1)} %dynamic-slice_bitcast_fusion.11), channel_id=1, source_target_pairs={{0,8},{8,0},{16,24},{24,16},{1,9},{9,1},{17,25},{25,17},{2,10},{10... | collective-permute-start | bytes 393224 | tf_op jit(solution)/shard_map/ppermute | solution.py:38
  375.4 8.4 %collective-permute-start.7 = (f32[64,512]{1,0:T(8,128)S(1)}, f32[64,512]{1,0:T(8,128)S(1)}, u32[]{:S(2)}, u32[]{:S(2)}) collective-permute-start(f32[64,512]{1,0:T(8,128)S(1)} %dynamic-slice_bitcast_fusion.12), channel_id=1, source_target_pairs={{0,16},{8,24},{16,0},{24,8},{1,17},{9,25},{17,1},{25,9},{2,18},{10... | collective-permute-start | bytes 393224 | tf_op jit(solution)/shard_map/ppermute | solution.py:38
  378.2 5.7 %collective-permute-start.5 = (f32[64,512]{1,0:T(8,128)S(1)}, f32[64,512]{1,0:T(8,128)S(1)}, u32[]{:S(2)}, u32[]{:S(2)}) collective-permute-start(f32[64,512]{1,0:T(8,128)S(1)} %dynamic-slice_bitcast_fusion.13), channel_id=1, source_target_pairs={{0,8},{8,0},{16,24},{24,16},{1,9},{9,1},{17,25},{25,17},{2,10},{10... | collective-permute-start | bytes 393224 | tf_op jit(solution)/shard_map/ppermute | solution.py:38
  379.7 6.3 %collective-permute-start.3 = (f32[64,512]{1,0:T(8,128)S(1)}, f32[64,512]{1,0:T(8,128)S(1)}, u32[]{:S(2)}, u32[]{:S(2)}) collective-permute-start(f32[64,512]{1,0:T(8,128)S(1)} %dynamic-slice_bitcast_fusion.14), channel_id=1, source_target_pairs={{0,16},{8,24},{16,0},{24,8},{1,17},{9,25},{17,1},{25,9},{2,18},{10... | collective-permute-start | bytes 393224 | tf_op jit(solution)/shard_map/ppermute | solution.py:38
  381.3 5.0 %collective-permute-start.1 = (f32[64,512]{1,0:T(8,128)S(1)}, f32[64,512]{1,0:T(8,128)S(1)}, u32[]{:S(2)}, u32[]{:S(2)}) collective-permute-start(f32[64,512]{1,0:T(8,128)S(1)} %dynamic-slice_bitcast_fusion.15), channel_id=1, source_target_pairs={{0,8},{8,0},{16,24},{24,16},{1,9},{9,1},{17,25},{25,17},{2,10},{10... | collective-permute-start | bytes 393224 | tf_op jit(solution)/shard_map/ppermute | solution.py:38
Sparse Core Ops, SparseCore 0:
  11.0 84.7 all-gather.10
  97.4 80.5 all-gather.8
  179.6 80.5 all-gather.6
  261.6 80.5 all-gather.4
  344.3 88.0 reduce-scatter.1
